TPU v7x, 128 devices: a whole 4x4x4 slice. The times are simulated.
128 devices in a mesh: dp: 16 (over x_lo, y, core), layer: 8 (over x_hi, z).
Axes of the slice: x: 4 (x_hi: 2, x_lo: 2; x = x_hi * 2 + x_lo), y: 4, z: 4, core: 2. Of those that a mesh axis runs over, the one named last changes fastest.
Arguments:
- activations: bfloat16 [4096, 8, 7168], P('dp', 'layer'), may hold values from -200 to 200
- labels: int32 [4096], P('dp'), may hold values from 0 to 511
- weights: float32 [7168, 8, 512], P('dp', 'layer'), may hold values from -0.0625 to 0.0625
- first_moment: float32 [7168, 8, 512], P('dp', 'layer'), may hold values from -0.00036621094 to 0.00036621094
- second_moment: float32 [7168, 8, 512], P('dp', 'layer'), may hold values from 2.1287373e-12 to 2.1287373e-11
Outputs:
- new_weights: float32 [7168, 8, 512], P('dp', 'layer')
- new_first: float32 [7168, 8, 512], P('dp', 'layer')
- new_second: float32 [7168, 8, 512], P('dp', 'layer')
- loss: float32 [], replicated
All inputs are finite; a program needn't handle non-finite values.
Results may differ from a plain program's by a relative error of at most 0.0014.
Values may be sent and summed in bfloat16 or wider, within the bound.
A program may use at most 128 MiB of HBM per device.

v0:
```python
import functools
import jax
import jax.numpy as jnp
from jax import lax
from jax.sharding import Mesh
from jax.sharding import PartitionSpec as P

STEP = 10
DP = ("dp_0", "dp_1", "dp_2")
LAYER = ("layer_0", "layer_1")
DP_LAYER = ("dp_0", "dp_1", "dp_2", "layer_0", "layer_1")


def one_axis_at_a_time(shard, axes):
    return functools.reduce(lax.psum, axes, shard)


def shards(activations, labels, weights, first_moment, second_moment):
    tok_rows = activations.shape[0]
    local_layers = activations.shape[1]
    tokens = tok_rows * lax.axis_size(DP)
    layers = local_layers * lax.axis_size(LAYER)
    width = weights.shape[2]
    low_weights = weights.astype(jnp.bfloat16)
    block = activations
    logits = jnp.einsum(
        "tlk,klc->ltc",
        block,
        lax.all_gather(low_weights, DP, axis=0, tiled=True),
        preferred_element_type=jnp.float32,
    )
    top = jnp.max(logits, axis=2, keepdims=True)
    exps = jnp.exp(logits - top)
    denom = jnp.sum(exps, axis=2, keepdims=True)
    classes = jnp.arange(width, dtype=jnp.int32)
    onehot = (labels[None, :, None] == classes[None, None, :]).astype(jnp.float32)
    picked = jnp.sum(logits * onehot, axis=2)
    local_loss = jnp.sum(top[:, :, 0] + jnp.log(denom[:, :, 0]) - picked)
    probs = exps / denom
    slope = ((probs - onehot) / tokens).astype(jnp.bfloat16)
    total = one_axis_at_a_time(local_loss, DP_LAYER)
    regrouped = lax.all_to_all(activations, DP, split_axis=2, concat_axis=0, tiled=True)
    block = regrouped
    grad = jnp.einsum(
        "tlk,ltc->klc",
        block,
        lax.all_gather(slope, DP, axis=1, tiled=True),
        preferred_element_type=jnp.float32,
    )
    local_square = jnp.sum(grad * grad)
    square = one_axis_at_a_time(local_square, DP_LAYER)
    loss = total / (tokens * layers)
    factor = jnp.minimum(1.0, 0.25 / jnp.sqrt(square + 1e-12))
    clipped = factor * grad
    new_first = 0.9 * first_moment + 0.1 * clipped
    new_second = 0.999 * second_moment + 0.001 * clipped * clipped
    new_weights = weights - 0.001 * (new_first / (1.0 - 0.9**STEP)) / (
        jnp.sqrt(new_second / (1.0 - 0.999**STEP)) + 1e-08
    )
    return (new_weights, new_first, new_second, loss)


def solution(mesh):
    finer = Mesh(
        mesh.devices.reshape(2, 4, 2, 2, 4), ("dp_0", "dp_1", "dp_2", "layer_0", "layer_1")
    )
    in_specs = (
        P(DP, LAYER, None),
        P(DP),
        P(DP, LAYER, None),
        P(DP, LAYER, None),
        P(DP, LAYER, None),
    )
    out_specs = (P(DP, LAYER, None), P(DP, LAYER, None), P(DP, LAYER, None), P())
    return jax.shard_map(
        shards, mesh=finer, in_specs=in_specs, out_specs=out_specs, check_vma=False
    )
```

profile of v0, /device:TPU:0, one launch (start us, length us, event | category | flops | bytes accessed | tf_op | source)
XLA Modules:
  0.0 261.6 jit_solution(9206150363318013744)
XLA Ops:
  7.2 2.0 copy.43
  9.3 50.6 %all-gather.4.cloned.1.call-done = bf16[7168,1,512]{2,0,1:T(8,128)(2,1)} async-done(((bf16[448,1,512]{2,0,1:T(8,128)(2,1)}), bf16[7168,1,512]{2,0,1:T(8,128)(2,1)}) %all-gather.4.cloned.1.call-update) | async-done | bytes 7340048 | tf_op jit(solution)/shard_map/all_gather | solution.py:29
  59.9 6.3 %fusion.8 = (f32[256]{0:T(256)S(1)}, f32[256,512]{1,0:T(8,128)S(1)}) fusion(bf16[7168,1,512]{2,0,1:T(8,128)(2,1)} %all-gather.4.cloned.1.call-done, bf16[256,1,7168]{2,0,1:T(8,128)(2,1)} %param.5), kind=kOutput, calls=%fused_computation.18 | convolution fusion | flops 1879179008 | bytes 11535360 | tf_op jit(solution)/shard_map/tlk,klc->ltc/dot_general | solution.py:26
  66.2 0.3 select_reduce_fusion
  66.5 0.9 multiply_convert_fusion
  67.5 16.4 %copy.25 = bf16[256,1,7168]{0,1,2:T(2,128)(2,1)} copy(bf16[256,1,7168]{2,0,1:T(8,128)(2,1)} %param.5) | data formatting | bytes 7340032 | tf_op args[0]
  83.8 0.5 broadcast.32
  84.4 38.4 %reduce.9 = bf16[7168,256]{1,0:T(8,128)(2,1)} reduce(bf16[7168,1,256]{2,1,0:T(2,128)(2,1)} %bitcast.33, bf16[]{:T(256)} %broadcast.32), dimensions={1}, to_apply=%bitcast.23.reduce_sub_computation | reduce | bytes 7340034
  122.8 10.3 %reshape.68 = bf16[16,2,57344]{2,1,0:T(2,128)(2,1)} reshape(bf16[7168,256]{1,0:T(8,128)(2,1)} %reduce.9) | data formatting | bytes 7340032
  133.1 49.6 %all_to_all.15 = bf16[16,2,57344]{2,1,0:T(2,128)(2,1)} all-to-all(bf16[16,2,57344]{2,1,0:T(2,128)(2,1)} %reshape.68), channel_id=1, replica_groups=mesh['dp_0'=2,'dp_1'=4,'dp_2'=2,'layer_0'=2,'layer_1'=4] {'dp_0','dp_1',..., dimensions={0} | all-to-all | bytes 7340032 | tf_op jit(solution)/shard_map/all_to_all | solution.py:42
  182.7 12.0 %reshape.69 = bf16[7168,1,256]{2,1,0:T(2,128)(2,1)} reshape(bf16[16,2,57344]{2,1,0:T(2,128)(2,1)} %all_to_all.15) | data formatting | bytes 7340032
  194.7 3.7 %copy.32 = bf16[256,1,7168]{0,2,1:T(8,128)(2,1)S(1)} copy(bf16[256,1,7168]{0,1,2:T(2,128)(2,1)} %bitcast.34) | data formatting | bytes 7340032
  198.4 2.3 copy.33
  200.7 0.6 subtract_reduce_fusion
  201.3 7.0 %multiply_reduce_fusion = (f32[]{:T(128)}, f32[512,448]{0,1:T(8,128)}) fusion(bf16[4096,448]{0,1:T(8,128)(2,1)} %bitcast.36, bf16[4096,512]{1,0:T(8,128)(2,1)} %all-gather.6.cloned.1.call-done), kind=kOutput, calls=%fused_computation.10 | convolution fusion | flops 1879506944 | bytes 8781828 | tf_op jit(solution)/shard_map/tlk,ltc->klc/dot_general | solution.py:44
  208.3 5.5 %all-reduce.4 = (f32[]{:T(128)}, f32[]{:T(128)}) all-reduce(f32[]{:T(128)} %get-tuple-element.33, f32[]{:T(128)} %subtract_reduce_fusion), channel_id=1, replica_groups=mesh['dp_0'=2,'dp_1'=4,'dp_2'=2,'layer_0'=2,'layer_1'=4] {'dp_0'}, use_global_device_ids=true, to_apply=%region_3.0 | all-reduce | flops 2 | bytes 16 | tf_op jit(solution)/shard_map/psum | solution.py:15
  213.9 9.2 %all-reduce.1 = (f32[]{:T(128)}, f32[]{:T(128)}) all-reduce(f32[]{:T(128)} %get-tuple-element.26, f32[]{:T(128)} %get-tuple-element.27), channel_id=1, replica_groups=mesh['dp_0'=2,'dp_1'=4,'dp_2'=2,'layer_0'=2,'layer_1'=4] {'dp_1'}, use_global_device_ids=true, to_apply=%region_4.0 | all-reduce | flops 2 | bytes 16 | tf_op jit(solution)/shard_map/psum | solution.py:15
  223.1 3.1 %all-reduce.3 = (f32[]{:T(128)}, f32[]{:T(128)}) all-reduce(f32[]{:T(128)} %get-tuple-element.20, f32[]{:T(128)} %get-tuple-element.21), channel_id=1, replica_groups=mesh['dp_0'=2,'dp_1'=4,'dp_2'=2,'layer_0'=2,'layer_1'=4] {'dp_2'}, use_global_device_ids=true, to_apply=%region_5.0 | all-reduce | flops 2 | bytes 16 | tf_op jit(solution)/shard_map/psum | solution.py:15
  226.2 7.0 %all-reduce.2 = (f32[]{:T(128)}, f32[]{:T(128)}) all-reduce(f32[]{:T(128)} %get-tuple-element.24, f32[]{:T(128)} %get-tuple-element.25), channel_id=1, replica_groups=mesh['dp_0'=2,'dp_1'=4,'dp_2'=2,'layer_0'=2,'layer_1'=4] {'layer_0'}, use_global_device_ids=true, to_apply=%region_6.0 | all-reduce | flops 2 | bytes 16 | tf_op jit(solution)/shard_map/psum | solution.py:15
  233.2 11.5 %all-reduce = (f32[]{:T(128)}, f32[]{:T(128)}) all-reduce(f32[]{:T(128)} %get-tuple-element.22, f32[]{:T(128)} %get-tuple-element.23), channel_id=1, replica_groups=mesh['dp_0'=2,'dp_1'=4,'dp_2'=2,'layer_0'=2,'layer_1'=4] {'layer_1'}, use_global_device_ids=true, to_apply=%region_7.0 | all-reduce | flops 2 | bytes 16 | tf_op jit(solution)/shard_map/psum | solution.py:15
  245.5 1.8 divide_subtract_fusion
  247.3 1.9 copy.29
  249.2 1.9 copy.30
  251.1 1.9 copy.31
  (13 shorter events, 0.1 us)
Async XLA Ops:
  7.2 52.7 %all-gather.4.cloned.1.call-start = ((), (), s32[]{:S(2)}) async-start(), calls=%async_computation.1 | async-start | bytes 7798784 | tf_op jit(solution)/shard_map/all_gather | solution.py:29
  9.2 57.0 %copy-start.3 = (s32[256]{0:T(256)S(1)}, s32[256]{0:T(256)}, u32[]{:S(2)}) copy-start(s32[256]{0:T(256)} %param.6) | copy-start | bytes 3076
  9.3 192.0 %all-gather.6.cloned.1.call-start = ((), (), s32[]{:S(2)}) async-start(), calls=%async_computation.2 | async-start | bytes 4456448 | tf_op jit(solution)/shard_map/all_gather | solution.py:47
  201.3 44.2 %copy-start = (f32[448,1,512]{2,1,0:T(1,128)S(1)}, f32[448,1,512]{2,1,0:T(1,128)}, u32[]{:S(2)}) copy-start(f32[448,1,512]{2,1,0:T(1,128)} %param.7) | copy-start | bytes 2752516
  201.3 44.2 %copy-start.1 = (f32[448,1,512]{2,1,0:T(1,128)S(1)}, f32[448,1,512]{2,1,0:T(1,128)}, u32[]{:S(2)}) copy-start(f32[448,1,512]{2,1,0:T(1,128)} %param.8) | copy-start | bytes 2752516
  201.3 44.2 %copy-start.2 = (f32[448,1,512]{2,1,0:T(1,128)S(1)}, f32[448,1,512]{2,1,0:T(1,128)}, u32[]{:S(2)}) copy-start(f32[448,1,512]{2,1,0:T(1,128)} %param.9) | copy-start | bytes 2752516
Sparse Core Ops, SparseCore 0:
  10.2 49.5 all-gather.3
  67.6 38.1 all-gather.5
where the time goes:
time: 263 us; the launch traced here: 262 us
  blocking collectives  86.1 us (33%)
  local copies, waits for them, and re-layouts  52.8 us (20%)
  waiting for transfers between devices  50.6 us (19%)
  other arithmetic  42.1 us (16%)
  between operations  16.6 us (6%)
  matrix products  13.3 us (5%)
    unnamed x18, local copies, waits for them, and re-layouts  52.8 us
    all_gather x1, waiting for transfers between devices, shards(): lax.all_gather(low_weights, DP, axis=0, tiled=True)  50.6 us
    all_to_all x1, blocking collectives, shards(): lax.all_to_all(activations, DP, split_axis=2, concat_axis=0, tiled=True)  49.6 us
    unnamed x1, other arithmetic  38.4 us
    psum x5, blocking collectives, one_axis_at_a_time(): return functools.reduce(lax.psum, axes, shard)  36.5 us
    dot_general x1, matrix products, shards(): jnp.einsum('tlk,ltc->klc', block, lax.all_gather(slope, DP, axis=1, tiled...  7.02 us
    dot_general x1, matrix products, shards(): jnp.einsum('tlk,klc->ltc', block, lax.all_gather(low_weights, DP, axis=0,...  6.33 us
  transfers between devices with their start and end apart: 2, of which 1 were waited for; matrix products, arithmetic and copies ran while one was open for 32% of the time, Pallas kernels for 0%

commit v1 on v0

--- a/solution.py
+++ b/solution.py
@@ -39,7 +39,9 @@
     probs = exps / denom
     slope = ((probs - onehot) / tokens).astype(jnp.bfloat16)
     total = one_axis_at_a_time(local_loss, DP_LAYER)
-    regrouped = lax.all_to_all(activations, DP, split_axis=2, concat_axis=0, tiled=True)
+    pieces = jnp.split(activations, lax.axis_size(DP), axis=2)
+    received = lax.all_to_all(jnp.stack(pieces), DP, 0, 0)
+    regrouped = jnp.concatenate(received, axis=0)
     block = regrouped
     grad = jnp.einsum(
         "tlk,ltc->klc",

time: 263 us -> 206 us (0.78)
  other arithmetic: 42.1 us -> 3.66 us
  local copies, waits for them, and re-layouts: 52.8 us -> 26 us
  blocking collectives: 86.1 us -> 95.2 us
    unnamed x1 -> x0, other arithmetic: 38.4 us -> none
    unnamed x18 -> x44, local copies, waits for them, and re-layouts: 52.8 us -> 21.7 us
    all_to_all x1, blocking collectives: 49.6 us -> 57.8 us  [shards(): received = lax.all_to_all(jnp.stack(pieces), DP, 0, 0)]
    split x0 -> x1, local copies, waits for them, and re-layouts: none -> 4.31 us  [shards(): pieces = jnp.split(activations, lax.axis_size(DP), axis=2)]
  transfers between devices with their start and end apart: 2 -> 2, of which waited for: 1 -> 1; matrix products, arithmetic and copies ran while one was open for 32% -> 9% of each run, Pallas kernels for 0% -> 0%
where the time goes in v1:
time: 206 us
  blocking collectives  95.2 us (46%)
  waiting for transfers between devices  50.6 us (25%)
  local copies, waits for them, and re-layouts  26 us (13%)
  between operations  16.8 us (8%)
  matrix products  13.4 us (7%)
  other arithmetic  3.66 us (2%)
    all_to_all x1, blocking collectives, shards(): received = lax.all_to_all(jnp.stack(pieces), DP, 0, 0)  57.8 us
    all_gather x1, waiting for transfers between devices, shards(): lax.all_gather(low_weights, DP, axis=0, tiled=True)  50.6 us
    psum x5, blocking collectives, one_axis_at_a_time(): return functools.reduce(lax.psum, axes, shard)  37.4 us
    unnamed x44, local copies, waits for them, and re-layouts  21.7 us
    dot_general x1, matrix products, shards(): jnp.einsum('tlk,ltc->klc', block, lax.all_gather(slope, DP, axis=1, tiled...  7.02 us
    dot_general x1, matrix products, shards(): jnp.einsum('tlk,klc->ltc', block, lax.all_gather(low_weights, DP, axis=0,...  6.33 us
    split x1, local copies, waits for them, and re-layouts, shards(): pieces = jnp.split(activations, lax.axis_size(DP), axis=2)  4.31 us
  transfers between devices with their start and end apart: 2, of which 1 were waited for; matrix products, arithmetic and copies ran while one was open for 9% of the time, Pallas kernels for 0%

profile of v1, /device:TPU:0, one launch (start us, length us, event | category | flops | bytes accessed | tf_op | source)
XLA Modules:
  0.0 205.7 jit_solution(8805954066591334002)
XLA Ops:
  7.2 2.0 copy.88
  9.3 50.6 %all-gather.4.cloned.1.call-done = bf16[7168,1,512]{2,0,1:T(8,128)(2,1)} async-done(((bf16[448,1,512]{2,0,1:T(8,128)(2,1)}), bf16[7168,1,512]{2,0,1:T(8,128)(2,1)}) %all-gather.4.cloned.1.call-update) | async-done | bytes 7340048 | tf_op jit(solution)/shard_map/all_gather | solution.py:29
  59.9 6.3 %fusion.9 = (f32[256]{0:T(256)S(1)}, f32[256,512]{1,0:T(8,128)S(1)}) fusion(bf16[7168,1,512]{2,0,1:T(8,128)(2,1)} %all-gather.4.cloned.1.call-done, bf16[256,1,7168]{2,0,1:T(8,128)(2,1)} %param.5), kind=kOutput, calls=%fused_computation.35 | convolution fusion | flops 1879179008 | bytes 11535360 | tf_op jit(solution)/shard_map/tlk,klc->ltc/dot_general | solution.py:26
  66.5 0.9 multiply_convert_fusion
  67.5 4.3 %fusion.8 = (bf16[256,1,448]{2,0,1:T(8,128)(2,1)S(1)}, bf16[256,1,448]{2,0,1:T(8,128)(2,1)S(1)}, bf16[256,1,448]{2,0,1:T(8,128)(2,1)S(1)}, bf16[256,1,448]{2,0,1...) fusion(bf16[256,1,7168]{2,0,1:T(8,128)(2,1)} %param.5), kind=kLoop, calls=%fused_computation.34 | loop fusion | bytes 7340032 | tf_op jit(solution)/shard_map/split | solution.py:42
  71.8 1.8 copy.62
  73.5 1.8 copy.63
  75.3 1.8 copy.64
  79.6 1.0 bitcast_dynamic-update-slice_fusion.15
  80.5 1.0 bitcast_dynamic-update-slice_fusion.14
  81.5 1.0 bitcast_dynamic-update-slice_fusion.13
  82.5 1.0 bitcast_dynamic-update-slice_fusion.12
  83.8 57.8 %all_to_all.5 = bf16[16,256,1,448]{1,3,2,0:T(8,128)(2,1)S(1)} all-to-all(bf16[16,256,1,448]{1,3,2,0:T(8,128)(2,1)S(1)} %bitcast_dynamic-update-slice_fusion), channel_id=1, replica_groups=mesh['dp_0'=2,'dp_1'=4,'dp_2'=2,'layer_0'=2,'layer_1'=4] {'dp_0','dp_1',..., dimensions={0} | all-to-all | bytes 7340032 | tf_op jit(solution)/shard_map/all_to_all | solution.py:43
  141.6 2.3 %copy.78 = bf16[56,8,16,256]{3,1,2,0:T(8,128)(2,1)} copy(bf16[56,8,16,256]{3,1,0,2:T(8,128)(2,1)S(1)} %bitcast.59) | data formatting | bytes 7340032
  144.5 7.0 %multiply_reduce_fusion = (f32[]{:T(128)}, f32[512,448]{0,1:T(8,128)}) fusion(bf16[4096,448]{0,1:T(8,128)(2,1)} %bitcast.60, bf16[4096,512]{1,0:T(8,128)(2,1)} %all-gather.6.cloned.1.call-done), kind=kOutput, calls=%fused_computation.10 | convolution fusion | flops 1879506944 | bytes 8781828 | tf_op jit(solution)/shard_map/tlk,ltc->klc/dot_general | solution.py:46
  151.5 5.5 %all-reduce.4 = (f32[]{:T(128)}, f32[]{:T(128)}) all-reduce(f32[]{:T(128)} %get-tuple-element.49, f32[]{:T(128)} %subtract_reduce_fusion), channel_id=1, replica_groups=mesh['dp_0'=2,'dp_1'=4,'dp_2'=2,'layer_0'=2,'layer_1'=4] {'dp_0'}, use_global_device_ids=true, to_apply=%region_3.0 | all-reduce | flops 2 | bytes 16 | tf_op jit(solution)/shard_map/psum | solution.py:15
  157.0 10.4 %all-reduce.1 = (f32[]{:T(128)}, f32[]{:T(128)}) all-reduce(f32[]{:T(128)} %get-tuple-element.26, f32[]{:T(128)} %get-tuple-element.27), channel_id=1, replica_groups=mesh['dp_0'=2,'dp_1'=4,'dp_2'=2,'layer_0'=2,'layer_1'=4] {'dp_1'}, use_global_device_ids=true, to_apply=%region_4.0 | all-reduce | flops 2 | bytes 16 | tf_op jit(solution)/shard_map/psum | solution.py:15
  167.4 3.1 %all-reduce.3 = (f32[]{:T(128)}, f32[]{:T(128)}) all-reduce(f32[]{:T(128)} %get-tuple-element.20, f32[]{:T(128)} %get-tuple-element.21), channel_id=1, replica_groups=mesh['dp_0'=2,'dp_1'=4,'dp_2'=2,'layer_0'=2,'layer_1'=4] {'dp_2'}, use_global_device_ids=true, to_apply=%region_5.0 | all-reduce | flops 2 | bytes 16 | tf_op jit(solution)/shard_map/psum | solution.py:15
  170.5 7.0 %all-reduce.2 = (f32[]{:T(128)}, f32[]{:T(128)}) all-reduce(f32[]{:T(128)} %get-tuple-element.24, f32[]{:T(128)} %get-tuple-element.25), channel_id=1, replica_groups=mesh['dp_0'=2,'dp_1'=4,'dp_2'=2,'layer_0'=2,'layer_1'=4] {'layer_0'}, use_global_device_ids=true, to_apply=%region_6.0 | all-reduce | flops 2 | bytes 16 | tf_op jit(solution)/shard_map/psum | solution.py:15
  177.6 11.4 %all-reduce = (f32[]{:T(128)}, f32[]{:T(128)}) all-reduce(f32[]{:T(128)} %get-tuple-element.22, f32[]{:T(128)} %get-tuple-element.23), channel_id=1, replica_groups=mesh['dp_0'=2,'dp_1'=4,'dp_2'=2,'layer_0'=2,'layer_1'=4] {'layer_1'}, use_global_device_ids=true, to_apply=%region_7.0 | all-reduce | flops 2 | bytes 16 | tf_op jit(solution)/shard_map/psum | solution.py:15
  189.7 1.8 divide_subtract_fusion
  191.5 1.9 copy.59
  193.3 1.9 copy.60
  195.2 1.9 copy.61
  (40 shorter events, 3.7 us)
Async XLA Ops:
  7.2 52.7 %all-gather.4.cloned.1.call-start = ((), (), s32[]{:S(2)}) async-start(), calls=%async_computation.1 | async-start | bytes 7798784 | tf_op jit(solution)/shard_map/all_gather | solution.py:29
  9.2 57.0 %copy-start.3 = (s32[256]{0:T(256)S(1)}, s32[256]{0:T(256)}, u32[]{:S(2)}) copy-start(s32[256]{0:T(256)} %param.6) | copy-start | bytes 3076
  9.3 135.2 %all-gather.6.cloned.1.call-start = ((), (), s32[]{:S(2)}) async-start(), calls=%async_computation.2 | async-start | bytes 4456448 | tf_op jit(solution)/shard_map/all_gather | solution.py:49
  144.5 45.2 %copy-start = (f32[448,1,512]{2,1,0:T(1,128)S(1)}, f32[448,1,512]{2,1,0:T(1,128)}, u32[]{:S(2)}) copy-start(f32[448,1,512]{2,1,0:T(1,128)} %param.7) | copy-start | bytes 2752516
  144.5 45.2 %copy-start.1 = (f32[448,1,512]{2,1,0:T(1,128)S(1)}, f32[448,1,512]{2,1,0:T(1,128)}, u32[]{:S(2)}) copy-start(f32[448,1,512]{2,1,0:T(1,128)} %param.8) | copy-start | bytes 2752516
  144.5 45.2 %copy-start.2 = (f32[448,1,512]{2,1,0:T(1,128)S(1)}, f32[448,1,512]{2,1,0:T(1,128)}, u32[]{:S(2)}) copy-start(f32[448,1,512]{2,1,0:T(1,128)} %param.9) | copy-start | bytes 2752516
Sparse Core Ops, SparseCore 0:
  10.2 49.5 all-gather.3
  67.6 71.4 all-gather.5
